TPU v7x, 32 devices: a whole 2x2x4 slice. The times are simulated.
32 devices in a mesh: row: 4 (over x, core), col: 8 (over z, y).
Axes of the slice: x: 2, y: 2, z: 4, core: 2. Of those that a mesh axis runs over, the one named last changes fastest.
Arguments:
- weight: bfloat16 [16384, 16384], P('row', 'col'), may hold values from -0.046875 to 0.046875
- momentum: float32 [16384, 16384], P('row', 'col'), may hold values from -36 to 36
- right_factor: float32 [16384, 512], P(('col', 'row')), may hold values from -0.046875 to 0.046875
- output_grads: bfloat16 [1024, 16384], P('col', 'row'), may hold values from -0.1875 to 0.1875
- activations: bfloat16 [1024, 16384], P('row', 'col'), may hold values from -6 to 6
Outputs:
- new_weight: bfloat16 [16384, 16384], P('row', 'col')
- new_momentum: float32 [16384, 16384], P('row', 'col')
- new_factor: float32 [16384, 512], P(('col', 'row'))
All inputs are finite; a program needn't handle non-finite values.
Results may differ from a plain program's by a relative error of at most 0.0004.
Values may be sent and summed in bfloat16 or wider, within the bound.
No kernel may reach another device: no remote copies, remote signals or barrier semaphores. Data moves between devices by JAX's collectives and lax.ppermute only.
A program may use at most 192 MiB of HBM per device.

v0:
```python
import math
import jax
import jax.numpy as jnp
from jax import lax
from jax.sharding import PartitionSpec as P

D_OUT = 16384
D_IN = 16384
FULL_PRECISION = lax.Precision.HIGHEST
MOMENTUM_DECAY = 0.95
LEARN_RATE = 0.002
NORM_EPS = 1e-06


def contract_rows(first, second):
    return lax.dot_general(
        first,
        second,
        (((0,), (0,)), ((), ())),
        precision=FULL_PRECISION,
        preferred_element_type=jnp.float32,
    )


def outer_rows(first, second):
    return lax.dot_general(
        first,
        second,
        (((1,), (1,)), ((), ())),
        precision=FULL_PRECISION,
        preferred_element_type=jnp.float32,
    )


def orthogonalize(left_factor, gram_matrix):
    lower_factor = jnp.linalg.cholesky(gram_matrix)
    identity = jnp.eye(gram_matrix.shape[0], dtype=gram_matrix.dtype)
    inverse = jax.scipy.linalg.solve_triangular(lower_factor, identity, lower=True)
    return outer_rows(left_factor, inverse)


def body(weight, momentum, right_factor, output_grads, activations):
    grads_whole = lax.all_gather(output_grads, "col", axis=0, tiled=True)
    grad_tile = lax.dot_general(
        grads_whole,
        lax.all_gather(activations, "row", axis=0, tiled=True),
        (((0,), (0,)), ((), ())),
        preferred_element_type=jnp.float32,
    )
    buffer = momentum + grad_tile
    factor_block = lax.all_gather(right_factor, "row", axis=0, tiled=True)
    left_partial = jnp.dot(
        buffer, factor_block, precision=FULL_PRECISION, preferred_element_type=jnp.float32
    )
    left_factor = lax.psum(left_partial, "col")
    gram_matrix = lax.psum(contract_rows(left_factor, left_factor), "row")
    ortho_left = orthogonalize(left_factor, gram_matrix)
    right_piece = lax.psum_scatter(
        contract_rows(buffer, ortho_left), "row", scatter_dimension=0, tiled=True
    )
    column_squares = lax.psum(jnp.sum(right_piece * right_piece, axis=0), ("row", "col"))
    column_norm = jnp.sqrt(column_squares + NORM_EPS)
    new_factor = right_piece / column_norm
    projected = lax.all_gather(right_piece, "row", axis=0, tiled=True)
    new_momentum = buffer - (1.0 - MOMENTUM_DECAY) * outer_rows(ortho_left, projected)
    factor_cols = projected / column_norm
    step_scale = LEARN_RATE * math.sqrt(max(D_OUT, D_IN))
    new_weight = (
        weight.astype(jnp.float32) - step_scale * outer_rows(ortho_left, factor_cols)
    ).astype(jnp.bfloat16)
    return (new_weight, new_momentum, new_factor)


def solution(mesh):
    in_specs = (
        P("row", "col"),
        P("row", "col"),
        P(("col", "row"), None),
        P("col", "row"),
        P("row", "col"),
    )
    out_specs = (P("row", "col"), P("row", "col"), P(("col", "row"), None))
    return jax.shard_map(body, mesh=mesh, in_specs=in_specs, out_specs=out_specs, check_vma=False)
```

profile of v0, /device:TPU:0, one launch (start us, length us, event | category | flops | bytes accessed | tf_op | source)
XLA Modules:
  0.0 1043.1 jit_solution(17681060143477142184)
XLA Ops:
  9.4 37.3 %all-gather.7.cloned.1.call-done = bf16[1024,2048]{1,0:T(8,128)(2,1)} async-done(((bf16[256,2048]{1,0:T(8,128)(2,1)}), bf16[1024,2048]{1,0:T(8,128)(2,1)}) %all-gather.7.cloned.1.call-update) | async-done | bytes 4194320 | tf_op jit(solution)/shard_map/all_gather | solution.py:46
  46.7 126.6 %all-gather.5.cloned.1.call-done = bf16[1024,4096]{1,0:T(8,128)(2,1)} async-done(((bf16[128,4096]{1,0:T(8,128)(2,1)}), bf16[1024,4096]{1,0:T(8,128)(2,1)}) %all-gather.5.cloned.1.call-update) | async-done | bytes 8388624 | tf_op jit(solution)/shard_map/all_gather | solution.py:43
  173.4 36.2 %convolution_add_fusion = f32[4096,2048]{1,0:T(8,128)} fusion(f32[4096,2048]{1,0:T(8,128)} %param.6, bf16[1024,4096]{1,0:T(8,128)(2,1)} %all-gather.5.cloned.1.call-done, bf16[1024,2048]{1,0:T(8,128)(2,1)} %all-gather.7.cloned.1.call-done), kind=kOutput, calls=%fused_computation.4 | convolution fusion | flops 17188257792 | bytes 79691776 | tf_op jit(solution)/shard_map/dot_general | solution.py:44
  209.6 65.1 %fusion.43 = f32[4096,512]{1,0:T(8,128)} fusion(f32[4096,2048]{1,0:T(8,128)} %convolution_add_fusion, f32[2048,512]{1,0:T(8,128)} %all-gather.9.cloned.1.call-done), kind=kOutput, calls=%fused_computation.85 | convolution fusion | flops 51539607552 | bytes 46137344 | tf_op jit(solution)/shard_map/dot_general | solution.py:52
  275.0 267.8 %all-reduce.4.cloned.1.call-done = f32[4096,512]{1,0:T(8,128)} async-done(((f32[4096,512]{1,0:T(8,128)}), f32[4096,512]{1,0:T(8,128)}) %all-reduce.4.cloned.1.call-update) | async-done | bytes 8388624 | tf_op jit(solution)/shard_map/psum | solution.py:55
  542.8 18.5 %fusion.44 = f32[512,512]{0,1:T(8,128)} fusion(f32[4096,512]{1,0:T(8,128)} %all-reduce.4.cloned.1.call-done), kind=kOutput, calls=%fused_computation.86 | convolution fusion | flops 12884901888 | bytes 9437184 | tf_op jit(solution)/shard_map/dot_general | solution.py:16
  562.3 34.6 %all-reduce.6.cloned.1.call-done = f32[512,512]{0,1:T(8,128)} async-done(((f32[512,512]{0,1:T(8,128)}), f32[512,512]{0,1:T(8,128)}) %all-reduce.6.cloned.1.call-update) | async-done | bytes 1048592 | tf_op jit(solution)/shard_map/psum | solution.py:56
  596.9 1.6 copy.9
  598.4 1.4 fusion.10
  599.9 11.7 %cholesky.104 = f32[128,128]{1,0:T(8,128)S(1)} custom-call(f32[128,128]{1,0:T(8,128)S(1)} %cholesky.266), custom_call_target="Cholesky" | custom-call | tf_op jit(solution)/shard_map/jit(cholesky)/cholesky | solution.py:36
  611.7 9.8 custom-call.31
  622.3 11.7 %cholesky.217 = f32[128,128]{1,0:T(8,128)S(1)} custom-call(f32[128,128]{1,0:T(8,128)S(1)} %cholesky.270), custom_call_target="Cholesky" | custom-call | tf_op jit(solution)/shard_map/jit(cholesky)/cholesky | solution.py:36
  634.0 18.5 %custom-call.32 = f32[1,128,128]{1,2,0:T(8,128)S(1)} custom-call(f32[1,128,128]{2,1,0:T(8,128)S(1)} %get-tuple-element.27), custom_call_target="InvertDiagBlocksLowerTriangular" | custom-call | tf_op jit(solution)/shard_map/jit(cholesky)/cholesky | solution.py:36
  653.2 11.7 %cholesky.238 = f32[128,128]{1,0:T(8,128)S(1)} custom-call(f32[128,128]{1,0:T(8,128)S(1)} %cholesky.275), custom_call_target="Cholesky" | custom-call | tf_op jit(solution)/shard_map/jit(cholesky)/cholesky | solution.py:36
  665.6 9.8 custom-call.33
  676.0 11.7 %cholesky.255 = f32[128,128]{1,0:T(8,128)S(1)} custom-call(f32[128,128]{1,0:T(8,128)S(1)} %convolution_subtract_fusion.5), custom_call_target="Cholesky" | custom-call | tf_op jit(solution)/shard_map/jit(cholesky)/cholesky | solution.py:36
  692.0 10.1 while.1
  692.6 1.9 bitcast_dynamic-update-slice_fusion.2
  695.1 1.9 bitcast_dynamic-update-slice_fusion.2
  697.6 1.9 bitcast_dynamic-update-slice_fusion.2
  700.2 1.9 bitcast_dynamic-update-slice_fusion.2
  702.1 40.1 %custom-call.34 = f32[4,128,128]{1,2,0:T(8,128)S(1)} custom-call(f32[4,128,128]{2,1,0:T(8,128)} %get-tuple-element.10), custom_call_target="InvertDiagBlocksLowerTriangular" | custom-call | tf_op jit(solution)/shard_map/jit(_solve_triangular)/triangular_solve | solution.py:38
  742.2 1.1 fusion.21
  746.0 17.1 %fusion.2 = f32[4096,512]{1,0:T(8,128)S(1)} fusion(f32[4096,512]{1,0:T(8,128)} %all-reduce.4.cloned.1.call-done, f32[128,512]{1,0:T(8,128)S(1)} %fusion.30, f32[128,512]{1,0:T(8,128)S(1)} %fusion.31, f32[128,512]{1,0:T(8,128)S(1)} %fusion.33, f32[128,512]{1,0:T(8,128)S(1)} %fusion.21), kind=kOutput, calls=%fused_computation.16 | convolution fusion | flops 12885688320 | bytes 17825792 | tf_op jit(solution)/shard_map/dot_general | solution.py:26
  763.2 3.2 copy-done
  766.4 58.7 %fusion.45 = f32[2048,512]{1,0:T(8,128)} fusion(f32[4096,2048]{1,0:T(8,128)} %convolution_add_fusion, f32[4096,512]{1,0:T(8,128)S(1)} %fusion.2), kind=kOutput, calls=%fused_computation.87 | convolution fusion | flops 51539607552 | bytes 46137344 | tf_op jit(solution)/shard_map/dot_general | solution.py:16
  825.2 45.2 %reduce-scatter.2.cloned.1.call-done = f32[512,512]{1,0:T(8,128)} async-done(((f32[2048,512]{1,0:T(8,128)}), f32[512,512]{1,0:T(8,128)}) %reduce-scatter.2.cloned.1.call-update) | async-done | bytes 1048592 | tf_op jit(solution)/shard_map/reduce_scatter | solution.py:58
  870.4 1.3 multiply_reduce_fusion
  871.7 39.7 %psum.23 = f32[512]{0:T(512)S(1)} all-reduce(f32[512]{0:T(512)S(1)} %multiply_reduce_fusion), channel_id=1, replica_groups=mesh['row'=4,'col'=8] {'row','col'}, use_global_device_ids=true, to_apply=%region_12.13 | all-reduce | flops 512 | bytes 4096 | tf_op jit(solution)/shard_map/psum | solution.py:61
  911.4 2.3 broadcast_divide_fusion
  913.8 62.5 %multiply_subtract_fusion = f32[4096,2048]{1,0:T(8,128)} fusion(f32[4096,2048]{1,0:T(8,128)} %convolution_add_fusion, f32[4096,512]{1,0:T(8,128)} %copy-done, f32[2048,512]{1,0:T(8,128)} %all-gather.11.cloned.1.call-done), kind=kOutput, calls=%fused_computation.2 | convolution fusion | flops 51556384768 | bytes 79691776 | tf_op jit(solution)/shard_map/dot_general | solution.py:26
  976.3 59.6 %subtract_convert_fusion = bf16[4096,2048]{1,0:T(8,128)(2,1)} fusion(bf16[4096,2048]{1,0:T(8,128)(2,1)} %param.5, f32[4096,512]{1,0:T(8,128)} %copy-done, f32[2048,512]{1,0:T(8,128)S(1)} %copy-done.1, f32[512]{0:T(512)S(1)} %add_sqrt_fusion), kind=kOutput, calls=%fused_computation.3 | convolution fusion | flops 51574210560 | bytes 46139392 | tf_op jit(solution)/shard_map/dot_general | solution.py:26
  (57 shorter events, 13.2 us)
Async XLA Ops:
  7.2 39.6 %all-gather.7.cloned.1.call-start = ((), (), s32[]{:S(2)}) async-start(), calls=%async_computation.2 | async-start | bytes 5242880 | tf_op jit(solution)/shard_map/all_gather | solution.py:46
  7.9 165.5 %all-gather.5.cloned.1.call-start = ((), (), s32[]{:S(2)}) async-start(), calls=%async_computation.1 | async-start | bytes 9437184 | tf_op jit(solution)/shard_map/all_gather | solution.py:43
  8.6 201.0 %all-gather.9.cloned.1.call-start = ((), (), s32[]{:S(2)}) async-start(), calls=%async_computation.3 | async-start | bytes 5242880 | tf_op jit(solution)/shard_map/all_gather | solution.py:51
  9.4 533.4 %all-reduce.4.cloned.1.call-start = ((), (), s32[]{:S(2)}) async-start(), calls=%async_computation.4 | async-start | bytes 16777216 | tf_op jit(solution)/shard_map/psum | solution.py:55
  274.7 322.2 %all-reduce.6.cloned.1.call-start = ((), (), s32[]{:S(2)}) async-start(), calls=%async_computation.5 | async-start | bytes 2097152 | tf_op jit(solution)/shard_map/psum | solution.py:56
  561.3 309.0 %reduce-scatter.2.cloned.1.call-start = ((), (), s32[]{:S(2)}) async-start(), calls=%async_computation.6 | async-start | bytes 5242880 | tf_op jit(solution)/shard_map/reduce_scatter | solution.py:58
  763.2 3.2 copy-start
  825.1 88.6 %all-gather.11.cloned.1.call-start = ((), (), s32[]{:S(2)}) async-start(), calls=%async_computation.7 | async-start | bytes 5242880 | tf_op jit(solution)/shard_map/all_gather | solution.py:64
  913.8 62.5 %copy-start.1 = (f32[2048,512]{1,0:T(8,128)S(1)}, f32[2048,512]{1,0:T(8,128)}, u32[]{:S(2)}) copy-start(f32[2048,512]{1,0:T(8,128)} %all-gather.11.cloned.1.call-done) | copy-start | bytes 12582916
Sparse Core Ops, SparseCore 0:
  9.5 37.1 all-gather.6
  48.9 124.4 all-gather.4
  174.9 32.6 all-gather.8
  274.8 267.9 all-reduce.3
  561.5 35.3 all-reduce.5
  825.3 45.0 reduce-scatter.1
  871.9 34.7 all-gather.10
where the time goes:
time: 1050 us; the launch traced here: 1040 us
  waiting for transfers between devices  514 us (49%)
  matrix products  323 us (31%)
  other arithmetic  134 us (13%)
  blocking collectives  39.7 us (4%)
  between operations  17.2 us (2%)
  local copies, waits for them, and re-layouts  15 us (1%)
    psum x1, waiting for transfers between devices, body(): left_factor = lax.psum(left_partial, 'col')  268 us
    dot_general x3, matrix products, outer_rows(): lax.dot_general(first, second, (((1,), (1,)), ((), ())), precision=FULL_P...  139 us
    all_gather x1, waiting for transfers between devices, body(): grads_whole = lax.all_gather(output_grads, 'col', axis=0, tiled=True)  127 us
    another operation x14, other arithmetic, orthogonalize(): lower_factor = jnp.linalg.cholesky(gram_matrix)  87.4 us
    dot_general x2, matrix products, contract_rows(): lax.dot_general(first, second, (((0,), (0,)), ((), ())), precision=FULL_P...  77.2 us
    dot_general x1, matrix products, body(): jnp.dot(buffer, factor_block, precision=FULL_PRECISION, preferred_element...  65.1 us
    reduce_scatter x1, waiting for transfers between devices, body(): lax.psum_scatter(contract_rows(buffer, ortho_left), 'row', scatter_dimens...  45.2 us
    another operation x3, other arithmetic, orthogonalize(): jax.scipy.linalg.solve_triangular(lower_factor, identity, lower=True)  40.3 us
  transfers between devices with their start and end apart: 7, of which 5 were waited for; matrix products, arithmetic and copies ran while one was open for 4% of the time, Pallas kernels for 0%

commit v1 on v0

--- a/solution.py
+++ b/solution.py
@@ -52,7 +52,11 @@
     left_partial = jnp.dot(
         buffer, factor_block, precision=FULL_PRECISION, preferred_element_type=jnp.float32
     )
-    left_factor = lax.psum(left_partial, "col")
+    left_factor = left_partial
+    for hop in (1, 2, 4):
+        left_factor = left_factor + lax.ppermute(
+            left_factor, "col", [(dev, dev ^ hop) for dev in range(8)]
+        )
     gram_matrix = lax.psum(contract_rows(left_factor, left_factor), "row")
     ortho_left = orthogonalize(left_factor, gram_matrix)
     right_piece = lax.psum_scatter(

time: 1050 us -> 1530 us (1.46)
  waiting for transfers between devices: 514 us -> 967 us
  other arithmetic: 134 us -> 159 us
    ppermute x0 -> x3, waiting for transfers between devices: none -> 720 us  [body(): lax.ppermute(left_factor, 'col', [(dev, dev ^ hop) for dev in range(8)])]
    psum x1 -> x0, waiting for transfers between devices: 268 us -> none  [body(): left_factor = lax.psum(left_partial, 'col')]
    add x0 -> x3, other arithmetic: none -> 33.8 us  [body(): left_factor + lax.ppermute(left_factor, 'col', [(dev, dev ^ hop) for dev...]
  transfers between devices with their start and end apart: 7 -> 9, of which waited for: 5 -> 7; matrix products, arithmetic and copies ran while one was open for 4% -> 3% of each run, Pallas kernels for 0% -> 0%
where the time goes in v1:
time: 1530 us; the launch traced here: 1520 us
  waiting for transfers between devices  967 us (63%)
  matrix products  316 us (21%)
  other arithmetic  159 us (10%)
  blocking collectives  39.7 us (3%)
  local copies, waits for them, and re-layouts  19.2 us (1%)
  between operations  17.3 us (1%)
    ppermute x3, waiting for transfers between devices, body(): lax.ppermute(left_factor, 'col', [(dev, dev ^ hop) for dev in range(8)])  720 us
    dot_general x3, matrix products, outer_rows(): lax.dot_general(first, second, (((1,), (1,)), ((), ())), precision=FULL_P...  139 us
    all_gather x1, waiting for transfers between devices, body(): grads_whole = lax.all_gather(output_grads, 'col', axis=0, tiled=True)  127 us
    another operation x14, other arithmetic, orthogonalize(): lower_factor = jnp.linalg.cholesky(gram_matrix)  79 us
    dot_general x2, matrix products, contract_rows(): lax.dot_general(first, second, (((0,), (0,)), ((), ())), precision=FULL_P...  77.1 us
    dot_general x1, matrix products, body(): jnp.dot(buffer, factor_block, precision=FULL_PRECISION, preferred_element...  58.1 us
    reduce_scatter x1, waiting for transfers between devices, body(): lax.psum_scatter(contract_rows(buffer, ortho_left), 'row', scatter_dimens...  45.2 us
    another operation x3, other arithmetic, orthogonalize(): jax.scipy.linalg.solve_triangular(lower_factor, identity, lower=True)  40.3 us
  transfers between devices with their start and end apart: 9, of which 7 were waited for; matrix products, arithmetic and copies ran while one was open for 3% of the time, Pallas kernels for 0%

profile of v1, /device:TPU:0, one launch (start us, length us, event | category | flops | bytes accessed | tf_op | source)
XLA Modules:
  0.0 1523.1 jit_solution(11734725807113835646)
XLA Ops:
  9.4 37.3 %all-gather.7.cloned.1.call-done = bf16[1024,2048]{1,0:T(8,128)(2,1)} async-done(((bf16[256,2048]{1,0:T(8,128)(2,1)}), bf16[1024,2048]{1,0:T(8,128)(2,1)}) %all-gather.7.cloned.1.call-update) | async-done | bytes 4194320 | tf_op jit(solution)/shard_map/all_gather | solution.py:46
  46.7 126.6 %all-gather.5.cloned.1.call-done = bf16[1024,4096]{1,0:T(8,128)(2,1)} async-done(((bf16[128,4096]{1,0:T(8,128)(2,1)}), bf16[1024,4096]{1,0:T(8,128)(2,1)}) %all-gather.5.cloned.1.call-update) | async-done | bytes 8388624 | tf_op jit(solution)/shard_map/all_gather | solution.py:43
  173.4 36.2 %convolution_add_fusion = f32[4096,2048]{1,0:T(8,128)} fusion(f32[4096,2048]{1,0:T(8,128)} %param.6, bf16[1024,4096]{1,0:T(8,128)(2,1)} %all-gather.5.cloned.1.call-done, bf16[1024,2048]{1,0:T(8,128)(2,1)} %all-gather.7.cloned.1.call-done), kind=kOutput, calls=%fused_computation.4 | convolution fusion | flops 17188257792 | bytes 79691776 | tf_op jit(solution)/shard_map/dot_general | solution.py:44
  209.6 58.1 %fusion.43 = f32[4096,512]{1,0:T(8,128)S(1)} fusion(f32[4096,2048]{1,0:T(8,128)} %convolution_add_fusion, f32[2048,512]{1,0:T(8,128)} %all-gather.9.cloned.1.call-done), kind=kOutput, calls=%fused_computation.85 | convolution fusion | flops 51539607552 | bytes 46137344 | tf_op jit(solution)/shard_map/dot_general | solution.py:52
  267.8 3.4 copy-done.1
  271.5 181.0 %collective-permute-done = f32[4096,512]{1,0:T(8,128)} collective-permute-done((f32[4096,512]{1,0:T(8,128)S(1)}, f32[4096,512]{1,0:T(8,128)}, u32[]{:S(2)}, u32[]{:S(2)}) %collective-permute-start) | collective-permute-done | bytes 8388640 | tf_op jit(solution)/shard_map/ppermute | solution.py:57
  452.5 11.3 add.66
  464.6 180.3 %collective-permute-done.1 = f32[4096,512]{1,0:T(8,128)} collective-permute-done((f32[4096,512]{1,0:T(8,128)}, f32[4096,512]{1,0:T(8,128)}, u32[]{:S(2)}, u32[]{:S(2)}) %collective-permute-start.1) | collective-permute-done | bytes 8388640 | tf_op jit(solution)/shard_map/ppermute | solution.py:57
  644.9 11.3 add.67
  656.2 2.4 collective-permute-start.2
  658.6 359.0 %collective-permute-done.2 = f32[4096,512]{1,0:T(8,128)} collective-permute-done((f32[4096,512]{1,0:T(8,128)}, f32[4096,512]{1,0:T(8,128)}, u32[]{:S(2)}, u32[]{:S(2)}) %collective-permute-start.2) | collective-permute-done | bytes 8388640 | tf_op jit(solution)/shard_map/ppermute | solution.py:57
  1017.5 11.3 add.68
  1028.8 18.4 %fusion.44 = f32[512,512]{0,1:T(8,128)} fusion(f32[4096,512]{1,0:T(8,128)} %add.68), kind=kOutput, calls=%fused_computation.86 | convolution fusion | flops 12884901888 | bytes 9437184 | tf_op jit(solution)/shard_map/dot_general | solution.py:16
  1048.6 35.8 %all-reduce.3.cloned.1.call-done = f32[512,512]{0,1:T(8,128)} async-done(((f32[512,512]{0,1:T(8,128)}), f32[512,512]{0,1:T(8,128)}) %all-reduce.3.cloned.1.call-update) | async-done | bytes 1048592 | tf_op jit(solution)/shard_map/psum | solution.py:60
  1087.4 11.7 cholesky.104
  1099.2 9.8 custom-call.31
  1109.8 11.7 cholesky.217
  1121.5 10.0 custom-call.32
  1132.2 11.7 cholesky.238
  1144.6 9.8 custom-call.33
  1155.1 11.7 cholesky.255
  1171.2 10.9 while.1
  1177.3 2.0 bitcast_dynamic-update-slice_fusion.2
  1182.0 40.1 %custom-call.34 = f32[4,128,128]{1,2,0:T(8,128)S(1)} custom-call(f32[4,128,128]{2,1,0:T(8,128)} %get-tuple-element.10), custom_call_target="InvertDiagBlocksLowerTriangular" | custom-call | tf_op jit(solution)/shard_map/jit(_solve_triangular)/triangular_solve | solution.py:38
  1226.0 17.1 %fusion.2 = f32[4096,512]{1,0:T(8,128)S(1)} fusion(f32[4096,512]{1,0:T(8,128)} %add.68, f32[128,512]{1,0:T(8,128)S(1)} %fusion.30, f32[128,512]{1,0:T(8,128)S(1)} %fusion.31, f32[128,512]{1,0:T(8,128)S(1)} %fusion.33, f32[128,512]{1,0:T(8,128)S(1)} %fusion.21), kind=kOutput, calls=%fused_computation.16 | convolution fusion | flops 12885688320 | bytes 17825792 | tf_op jit(solution)/shard_map/dot_general | solution.py:26
  1243.1 3.2 copy-done
  1246.3 58.7 %fusion.45 = f32[2048,512]{1,0:T(8,128)} fusion(f32[4096,2048]{1,0:T(8,128)} %convolution_add_fusion, f32[4096,512]{1,0:T(8,128)S(1)} %fusion.2), kind=kOutput, calls=%fused_computation.87 | convolution fusion | flops 51539607552 | bytes 46137344 | tf_op jit(solution)/shard_map/dot_general | solution.py:16
  1305.2 45.2 %reduce-scatter.2.cloned.1.call-done = f32[512,512]{1,0:T(8,128)} async-done(((f32[2048,512]{1,0:T(8,128)}), f32[512,512]{1,0:T(8,128)}) %reduce-scatter.2.cloned.1.call-update) | async-done | bytes 1048592 | tf_op jit(solution)/shard_map/reduce_scatter | solution.py:62
  1351.7 39.7 %psum.15 = f32[512]{0:T(512)S(1)} all-reduce(f32[512]{0:T(512)S(1)} %multiply_reduce_fusion), channel_id=1, replica_groups=mesh['row'=4,'col'=8] {'row','col'}, use_global_device_ids=true, to_apply=%region_11.12 | all-reduce | flops 512 | bytes 4096 | tf_op jit(solution)/shard_map/psum | solution.py:65
  1391.3 2.3 broadcast_divide_fusion
  1393.7 62.5 %multiply_subtract_fusion = f32[4096,2048]{1,0:T(8,128)} fusion(f32[4096,2048]{1,0:T(8,128)} %convolution_add_fusion, f32[4096,512]{1,0:T(8,128)} %copy-done, f32[2048,512]{1,0:T(8,128)} %all-gather.11.cloned.1.call-done), kind=kOutput, calls=%fused_computation.2 | convolution fusion | flops 51556384768 | bytes 79691776 | tf_op jit(solution)/shard_map/dot_general | solution.py:26
  1456.2 59.6 %subtract_convert_fusion = bf16[4096,2048]{1,0:T(8,128)(2,1)} fusion(bf16[4096,2048]{1,0:T(8,128)(2,1)} %param.5, f32[4096,512]{1,0:T(8,128)} %copy-done, f32[2048,512]{1,0:T(8,128)S(1)} %copy-done.2, f32[512]{0:T(512)S(1)} %add_sqrt_fusion), kind=kOutput, calls=%fused_computation.3 | convolution fusion | flops 51574210560 | bytes 46139392 | tf_op jit(solution)/shard_map/dot_general | solution.py:26
  (65 shorter events, 26.4 us)
Async XLA Ops:
  7.2 39.6 %all-gather.7.cloned.1.call-start = ((), (), s32[]{:S(2)}) async-start(), calls=%async_computation.2 | async-start | bytes 5242880 | tf_op jit(solution)/shard_map/all_gather | solution.py:46
  7.9 165.5 %all-gather.5.cloned.1.call-start = ((), (), s32[]{:S(2)}) async-start(), calls=%async_computation.1 | async-start | bytes 9437184 | tf_op jit(solution)/shard_map/all_gather | solution.py:43
  8.6 201.0 %all-gather.9.cloned.1.call-start = ((), (), s32[]{:S(2)}) async-start(), calls=%async_computation.3 | async-start | bytes 5242880 | tf_op jit(solution)/shard_map/all_gather | solution.py:51
  9.4 1075.0 %all-reduce.3.cloned.1.call-start = ((), (), s32[]{:S(2)}) async-start(), calls=%async_computation.4 | async-start | bytes 2097152 | tf_op jit(solution)/shard_map/psum | solution.py:60
  267.7 3.4 copy-start.1
  271.1 181.3 %collective-permute-start = (f32[4096,512]{1,0:T(8,128)S(1)}, f32[4096,512]{1,0:T(8,128)}, u32[]{:S(2)}, u32[]{:S(2)}) collective-permute-start(f32[4096,512]{1,0:T(8,128)S(1)} %fusion.43), channel_id=1, source_target_pairs={{0,1},{1,0},{2,3},{3,2},{4,5},{5,4},{6,7},{7,6},{8,9},{9,8},{10,11... | collective-permute-start | bytes 25165832 | tf_op jit(solution)/shard_map/ppermute | solution.py:57
  463.7 181.2 %collective-permute-start.1 = (f32[4096,512]{1,0:T(8,128)}, f32[4096,512]{1,0:T(8,128)}, u32[]{:S(2)}, u32[]{:S(2)}) collective-permute-start(f32[4096,512]{1,0:T(8,128)} %add.66), channel_id=1, source_target_pairs={{0,2},{1,3},{2,0},{3,1},{4,6},{5,7},{6,4},{7,5},{8,10},{9,11},{10,... | collective-permute-start | bytes 25165832 | tf_op jit(solution)/shard_map/ppermute | solution.py:57
  656.2 361.4 %collective-permute-start.2 = (f32[4096,512]{1,0:T(8,128)}, f32[4096,512]{1,0:T(8,128)}, u32[]{:S(2)}, u32[]{:S(2)}) collective-permute-start(f32[4096,512]{1,0:T(8,128)} %add.67), channel_id=1, source_target_pairs={{0,4},{1,5},{2,6},{3,7},{4,0},{5,1},{6,2},{7,3},{8,12},{9,13},{10,... | collective-permute-start | bytes 25165832 | tf_op jit(solution)/shard_map/ppermute | solution.py:57
  1047.2 303.1 %reduce-scatter.2.cloned.1.call-start = ((), (), s32[]{:S(2)}) async-start(), calls=%async_computation.5 | async-start | bytes 5242880 | tf_op jit(solution)/shard_map/reduce_scatter | solution.py:62
  1243.1 3.2 copy-start
  1305.1 88.6 %all-gather.11.cloned.1.call-start = ((), (), s32[]{:S(2)}) async-start(), calls=%async_computation.6 | async-start | bytes 5242880 | tf_op jit(solution)/shard_map/all_gather | solution.py:68
  1393.7 62.5 %copy-start.2 = (f32[2048,512]{1,0:T(8,128)S(1)}, f32[2048,512]{1,0:T(8,128)}, u32[]{:S(2)}) copy-start(f32[2048,512]{1,0:T(8,128)} %all-gather.11.cloned.1.call-done) | copy-start | bytes 12582916
Sparse Core Ops, SparseCore 0:
  9.5 37.1 all-gather.6
  48.9 124.4 all-gather.4
  174.9 32.6 all-gather.8
  1047.3 37.0 all-reduce.2
  1305.2 45.0 reduce-scatter.1
  1351.7 34.7 all-gather.10
